TPU v7x, 32 devices: a whole 2x2x4 slice. The times are simulated.
32 devices in a mesh: section: 4 (over z), expert: 4 (over y, core), seq: 2 (over x).
Axes of the slice: x: 2, y: 2, z: 4, core: 2. Of those that a mesh axis runs over, the one named last changes fastest.
Arguments:
- tokens: bfloat16 [512, 4096], P('expert', 'section'), may hold values from -6 to 6
- route_ids: int32 [512, 2], P('expert'), may hold values from 0 to 3, all different within a row; in each aligned block of 128 rows (0 to 127, 128 to 255, ...) at most 96 rows name the same one
- route_weights: float32 [512, 2], P('expert'), may hold values from 0.25 to 1
- gate_weight: bfloat16 [4, 4096, 8192], P('expert', None, ('section', 'seq')), may hold values from -0.09375 to 0.09375
- up_weight: bfloat16 [4, 4096, 8192], P('expert', None, ('section', 'seq')), may hold values from -0.09375 to 0.09375
- down_weight: bfloat16 [4, 8192, 4096], P('expert', 'section', 'seq'), may hold values from -0.0625 to 0.0625
Outputs:
- mixed: bfloat16 [512, 4096], P('expert', 'seq')
Inputs may be any that keep to these rules, and one draw needn't show every extreme that they name: `route_ids`: the two ids of a token differ; among the 128 tokens of one source group (held on one index of the expert axis) no expert is named more than 96 times.
All inputs are finite; a program needn't handle non-finite values.
Results may differ from a plain program's by a relative error of at most 0.0057.
Values may be sent and summed in bfloat16 or wider, within the bound.
A program may use at most 64 MiB of HBM per device.

v0:
```python
import functools

import jax
import jax.numpy as jnp
from jax import lax
from jax.experimental import pallas as pl
from jax.experimental.pallas import tpu as pltpu
from jax.sharding import PartitionSpec as P

MESH = pl.DeviceIdType.MESH


def plain(tokens, route_ids, route_weights, gate_weight, up_weight, down_weight):
    experts = lax.axis_size("expert")
    tok_rows, top_count = route_ids.shape
    capacity = 3 * tok_rows * top_count // (2 * experts)
    rows_total = experts * capacity
    flat_ids = route_ids.reshape(-1)
    onehot = (flat_ids[:, None] == jnp.arange(experts, dtype=jnp.int32)[None, :]).astype(jnp.int32)
    earlier = jnp.cumsum(onehot, axis=0) - onehot
    slot_index = jnp.sum(earlier * onehot, axis=1)
    destination = flat_ids * capacity + slot_index
    matches = (jnp.arange(rows_total, dtype=jnp.int32)[:, None] == destination[None, :]).astype(
        jnp.bfloat16
    )
    dispatch = jnp.sum(matches.reshape(rows_total, tok_rows, top_count), axis=2)
    outgoing = jnp.dot(dispatch, tokens, preferred_element_type=jnp.float32).astype(jnp.bfloat16)
    received = lax.all_to_all(
        outgoing.reshape(experts, capacity, tokens.shape[1]),
        "expert",
        split_axis=0,
        concat_axis=0,
        tiled=True,
    )
    received = received.reshape(rows_total, tokens.shape[1])
    piece = lax.all_gather(received, "section", axis=1, tiled=True)
    gate = jnp.dot(piece, gate_weight[0], preferred_element_type=jnp.float32)
    up = jnp.dot(piece, up_weight[0], preferred_element_type=jnp.float32)
    hidden = (jax.nn.silu(gate) * up).astype(jnp.bfloat16)
    partial_value = jnp.dot(
        lax.all_gather(hidden, "seq", axis=1, tiled=True),
        down_weight[0],
        preferred_element_type=jnp.float32,
    )
    summed = lax.psum_scatter(partial_value, "section", scatter_dimension=1, tiled=True)
    expert_out = summed.astype(jnp.bfloat16).reshape(experts, capacity, summed.shape[1])
    returned = lax.all_to_all(
        expert_out, "expert", split_axis=0, concat_axis=0, tiled=True
    ).reshape(rows_total, summed.shape[1])
    picked = (
        jnp.take(returned, destination, axis=0)
        .astype(jnp.float32)
        .reshape(tok_rows, top_count, summed.shape[1])
    )
    mixed = jnp.sum(picked * route_weights[:, :, None], axis=1).astype(jnp.bfloat16)
    return lax.all_gather(mixed, "section", axis=1, tiled=True)


def kernel(
    S, E, top, cap,
    tok_hbm, route_hbm, gate_hbm, up_hbm, down_hbm, out_ref,
    T, R, WG, WU, WD, DISP, WR, X, G, U, HO, HX, PO, CS, CR, YS, YR, ZS, ZR, AG,
    lsem, tsem, ssem, rsem, rrsem, hsem, csem, ysem, zsem, asem,
):
    s = lax.axis_index("section")
    e = lax.axis_index("expert")
    q = lax.axis_index("seq")
    core = e + 1 - 2 * lax.rem(e, 2)
    oy = lax.rem(e + 2, E)
    oyc = lax.rem(core + 2, E)
    oq = 1 - q
    rows = tok_hbm.shape[0]
    half = rows // 2
    feat = tok_hbm.shape[1]
    units = gate_hbm.shape[2]
    outs = down_hbm.shape[2]
    counter = [0]
    pending = []

    own = pltpu.make_async_copy(tok_hbm, T.at[s, pl.ds(pl.multiple_of(e * rows, rows), rows)], tsem.at[0])
    own.start()
    route = pltpu.make_async_copy(route_hbm, R.at[e], tsem.at[1])
    route.start()

    barrier = pltpu.get_barrier_semaphore()
    partners = [{"section": lax.rem(s + j, S)} for j in range(1, S)]
    partners += [{"expert": core}, {"expert": oy}, {"expert": oyc}, {"seq": oq}]
    for p in partners:
        pl.semaphore_signal(barrier, inc=1, device_id=p, device_id_type=MESH)

    order = [0, 1, S - 1] + list(range(2, S - 1))
    loads = {}
    for i, j in enumerate(order):
        k = lax.rem(s + j, S)
        band = pl.ds(pl.multiple_of(k * feat, feat), feat)
        loads[j] = (
            pltpu.make_async_copy(gate_hbm.at[0, band], WG.at[band], lsem.at[2 * i]),
            pltpu.make_async_copy(up_hbm.at[0, band], WU.at[band], lsem.at[2 * i + 1]),
        )
    down_load = pltpu.make_async_copy(down_hbm.at[0], WD, lsem.at[2 * S])

    own.wait()
    route.wait()
    pl.semaphore_wait(barrier, len(partners))

    def send(src, dst, recv, target):
        c = pltpu.make_async_remote_copy(
            src_ref=src, dst_ref=dst, send_sem=ssem.at[counter[0]], recv_sem=recv,
            device_id=target, device_id_type=MESH,
        )
        counter[0] += 1
        pending.append(c)
        c.start()

    def arrived(ref, sem):
        pltpu.make_async_remote_copy(
            src_ref=ref, dst_ref=ref, send_sem=ssem.at[0], recv_sem=sem,
            device_id={"seq": oq}, device_id_type=MESH,
        ).wait_recv()

    def chunk(group, part, k):
        return T.at[k, pl.ds(pl.multiple_of(group * rows + part * half, half), half)]

    def slot(group, part, k):
        return rsem.at[(group * 2 + part) * S + k]

    def push(group, part, k, *targets):
        for t in targets:
            send(chunk(group, part, k), chunk(group, part, k), slot(group, part, k), t)

    def take(group, part, k):
        arrived(chunk(group, part, k), slot(group, part, k))

    to_x, to_y, to_core = {"seq": oq}, {"expert": oy}, {"expert": core}
    sec = [lax.rem(s + j, S) for j in range(S)]
    for j in order[1:]:
        push(e, q, s, {"section": sec[j]})
    for t, target in enumerate((core, oy, oyc)):
        send(R.at[e], R.at[e], rrsem.at[e], {"expert": target})
    push(e, q, s, to_y, to_core)
    push(e, oq, s, to_y, to_core)
    for j in order:
        for c in loads[j]:
            c.start()
    down_load.start()

    def from_z(j):
        take(e, q, sec[j])
        push(e, q, sec[j], to_x, to_y, to_core)

    def from_x(j, on):
        take(e, oq, sec[j])
        push(e, oq, sec[j], to_core, *([to_y] if on else []))

    def from_y(j, on):
        take(oy, q, sec[j])
        push(oy, q, sec[j], *([to_x] if on else []), to_core)

    def from_diag(j):
        take(oy, oq, sec[j])
        push(oy, oq, sec[j], to_core)

    def from_core(j):
        for group in (core, oyc):
            for part in (0, 1):
                take(group, part, sec[j])

    tile = min(256, units)

    def section_matmul(j, first, spans=None, then=None):
        from_core(j)
        for c in loads[j]:
            c.wait()
        k = sec[j]
        for g in range(E):
            X[g * cap : (g + 1) * cap, :] = jnp.dot(
                DISP[g], T[k, g * rows : (g + 1) * rows, :], preferred_element_type=jnp.float32
            ).astype(jnp.bfloat16)
        band = pl.ds(pl.multiple_of(k * feat, feat), feat)

        for n_span, r in enumerate(spans or [slice(None)]):

            @pl.loop(0, units // tile)
            def _(n):
                cols = pl.ds(pl.multiple_of(n * tile, tile), tile)
                for W, A in ((WG, G), (WU, U)):
                    v = jnp.dot(X[r, :], W[band, cols], preferred_element_type=jnp.float32)
                    if first:
                        A[r, cols] = v
                    else:
                        A[r, cols] = A[r, cols] + v

            if then is not None:
                then(n_span)

    for g in (core, oy, oyc):
        arrived(R.at[g], rrsem.at[g])
    me = e.astype(jnp.float32)
    before = (
        lax.broadcasted_iota(jnp.int32, (rows, rows), 0) < lax.broadcasted_iota(jnp.int32, (rows, rows), 1)
    ).astype(jnp.float32).astype(jnp.bfloat16)
    for g in range(E):
        table = R[g]
        named = jnp.zeros((1, rows), jnp.float32)
        weight = jnp.zeros((1, rows), jnp.float32)
        for n in range(top):
            hit = (table[n : n + 1, :] == me).astype(jnp.float32)
            named = named + hit
            weight = weight + hit * table[top + n : top + n + 1, :]
        rank = jnp.dot(
            jnp.broadcast_to(named, (8, rows)).astype(jnp.bfloat16), before, preferred_element_type=jnp.float32
        )[0:1, :]
        place = lax.broadcasted_iota(jnp.int32, (cap, rows), 0).astype(jnp.float32)
        match = jnp.where(place == rank, 1.0, 0.0) * named
        DISP[g] = match.astype(jnp.bfloat16)
        WR[g] = jnp.broadcast_to(jnp.sum(match * weight, axis=1, keepdims=True), (cap, WR.shape[2]))

    from_z(order[1])
    take(oy, q, s)
    take(oy, oq, s)
    push(oy, q, s, to_core)
    push(oy, oq, s, to_core)
    others = order[1:]
    onward = {j: i < (S - 2) // 2 for i, j in enumerate(others)}
    for i, j in enumerate(others):
        if i + 1 < len(others):
            from_z(others[i + 1])
        from_x(j, onward[j])
        from_y(j, not onward[j])
        if i > 0:
            from_diag(others[i - 1])
        if i == len(others) - 2:
            section_matmul(0, True)
    for j in others[:-1]:
        section_matmul(j, False)
    from_diag(others[-1])
    groups = [oyc, oy, core, e]

    def span(g):
        return pl.ds(pl.multiple_of(g * cap, cap), cap)

    def hidden_out(n_span):
        for i in (2 * n_span, 2 * n_span + 1):
            g = groups[i]
            a = G[span(g), 0:units]
            HO[span(g), :] = (a / (1.0 + jnp.exp(-a)) * U[span(g), :]).astype(jnp.bfloat16)
            send(HO.at[span(g)], HX.at[span(g)], hsem.at[i], to_x)

    def chip_span(y):
        return pl.ds(pl.multiple_of(y * 2 * cap, 2 * cap), 2 * cap)

    section_matmul(others[-1], False, [chip_span(oy // 2), chip_span(e // 2)], hidden_out)

    down_load.wait()
    own_units = pl.ds(pl.multiple_of(q * units, units), units)
    other_units = pl.ds(pl.multiple_of(oq * units, units), units)
    otile = min(256, outs)

    @pl.loop(0, outs // otile)
    def _(n):
        cols = pl.ds(pl.multiple_of(n * otile, otile), otile)
        PO[:, cols] = jnp.dot(HO[...], WD[own_units, cols], preferred_element_type=jnp.float32)

    quarter = rows // S

    def lines(k):
        return pl.ds(pl.multiple_of(k * quarter, quarter), quarter)

    for i, g in enumerate(groups):
        arrived(HX.at[span(g)], hsem.at[i])
        if i == 1:
            arrived(CR.at[0], csem.at[0])
        if i == 3:
            arrived(CR.at[1], csem.at[1])

        @pl.loop(0, outs // otile)
        def _(n):
            cols = pl.ds(pl.multiple_of(n * otile, otile), otile)
            v = PO[span(g), cols] + jnp.dot(
                HX[span(g), :], WD[other_units, cols], preferred_element_type=jnp.float32
            )
            v = (v * WR[g][:, 0:1]).astype(jnp.bfloat16)
            v = lax.dot_general(DISP[g], v, (((0,), (0,)), ((), ())), preferred_element_type=jnp.float32)
            if i % 2 == 0:
                CS[i // 2, :, cols] = v.astype(jnp.bfloat16)
            elif i == 1:
                YS[:, cols] = (v + CR[0, :, cols].astype(jnp.float32)).astype(jnp.bfloat16)
            else:
                G[0:rows, cols] = v + CR[1, :, cols].astype(jnp.float32)

        if i % 2 == 0:
            send(CS.at[i // 2], CR.at[i // 2], csem.at[i // 2], to_core)
        elif i == 1:
            for j in others + [0]:
                send(YS.at[lines(sec[j])], YR.at[lines(sec[j])], ysem.at[j], to_y)

    def joined(j):
        arrived(YR.at[lines(sec[j])], ysem.at[j])
        return G[lines(sec[j]), 0:outs] + YR[lines(sec[j]), :].astype(jnp.float32)

    for j in others:
        ZS[lines(sec[j]), :] = joined(j).astype(jnp.bfloat16)
        send(ZS.at[lines(sec[j])], ZR.at[s], zsem.at[s], {"section": sec[j]})
    total = joined(0)
    for j in order[1:]:
        arrived(ZR.at[sec[j]], zsem.at[sec[j]])
    for j in order[1:]:
        total = total + ZR[sec[j]].astype(jnp.float32)
    AG[lines(s), :] = total.astype(jnp.bfloat16)
    for j in order[1:]:
        send(AG.at[lines(s)], AG.at[lines(s)], asem.at[s], {"section": sec[j]})
    for j in order[1:]:
        arrived(AG.at[lines(sec[j])], asem.at[sec[j]])
    out_ref[...] = AG[...]
    for c in pending:
        c.wait_send()


def fused(tokens, route_ids, route_weights, gate_weight, up_weight, down_weight):
    S, E = lax.axis_size("section"), lax.axis_size("expert")
    rows, feat = tokens.shape
    top = route_ids.shape[1]
    cap = 3 * rows * top // (2 * E)
    units, outs = gate_weight.shape[2], down_weight.shape[2]
    table = jnp.concatenate([route_ids.T.astype(jnp.float32), route_weights.T], axis=0)
    table = jnp.pad(table, ((0, -table.shape[0] % 8), (0, 0)))
    bf, f32 = jnp.bfloat16, jnp.float32
    dma = pltpu.SemaphoreType.DMA
    sends = 128
    return pl.pallas_call(
        functools.partial(kernel, S, E, top, cap),
        out_shape=jax.ShapeDtypeStruct((rows, outs), bf),
        in_specs=[pl.BlockSpec(memory_space=pl.ANY)] * 5,
        out_specs=pl.BlockSpec(memory_space=pltpu.VMEM),
        scratch_shapes=[
            pltpu.VMEM((S, E * rows, feat), bf),
            pltpu.VMEM((E,) + table.shape, f32),
            pltpu.VMEM((S * feat, units), bf),
            pltpu.VMEM((S * feat, units), bf),
            pltpu.VMEM(down_weight.shape[1:], bf),
            pltpu.VMEM((E, cap, rows), bf),
            pltpu.VMEM((E, cap, 128), f32),
            pltpu.VMEM((E * cap, feat), bf),
            pltpu.VMEM((E * cap, max(units, outs)), f32),
            pltpu.VMEM((E * cap, units), f32),
            pltpu.VMEM((E * cap, units), bf),
            pltpu.VMEM((E * cap, units), bf),
            pltpu.VMEM((E * cap, outs), f32),
            pltpu.VMEM((2, rows, outs), bf),
            pltpu.VMEM((2, rows, outs), bf),
            pltpu.VMEM((rows, outs), bf),
            pltpu.VMEM((rows, outs), bf),
            pltpu.VMEM((rows, outs), bf),
            pltpu.VMEM((S, rows // S, outs), bf),
            pltpu.VMEM((rows, outs), bf),
            dma((2 * S + 1,)),
            dma((2,)),
            dma((sends,)),
            dma((2 * E * S,)),
            dma((E,)),
            dma((4,)),
            dma((2,)),
            dma((S,)),
            dma((S,)),
            dma((S,)),
        ],
        compiler_params=pltpu.CompilerParams(
            collective_id=0, has_side_effects=True, vmem_limit_bytes=60 * 1024 * 1024
        ),
    )(tokens, table, gate_weight, up_weight, down_weight)


def shards(tokens, route_ids, route_weights, gate_weight, up_weight, down_weight):
    args = (tokens, route_ids, route_weights, gate_weight, up_weight, down_weight)
    pairs = lax.axis_size("expert") == 2 * 2 and lax.axis_size("seq") == 2
    if pairs and lax.axis_size("section") > 2:
        return fused(*args)
    return plain(*args)


def solution(mesh):
    in_specs = (
        P("expert", "section"),
        P("expert", None),
        P("expert", None),
        P("expert", None, ("section", "seq")),
        P("expert", None, ("section", "seq")),
        P("expert", "section", "seq"),
    )
    out_specs = P("expert", "seq")
    return jax.shard_map(shards, mesh=mesh, in_specs=in_specs, out_specs=out_specs, check_vma=False)
```

profile of v0, /device:TPU:2, one launch (start us, length us, event | category | flops | bytes accessed | tf_op | source)
XLA Modules:
  0.0 88.1 jit_solution(5911827565403590907)
XLA Ops:
  0.0 0.7 convert_bitcast_fusion
  0.7 1.3 %select_maximum_fusion.route_hbm = f32[8,128]{1,0:T(8,128)} fusion(f32[2,128]{1,0:T(2,128)} %bitcast.3, f32[2,128]{1,0:T(2,128)S(1)} %convert_bitcast_fusion), kind=kLoop, calls=%fused_computation | loop fusion | flops 4096 | bytes 6144 | tf_op jit(solution)/shard_map/concatenate | solution.py:325
  2.0 84.2 %shard_map.64 = bf16[128,2048]{1,0:T(8,128)(2,1)} custom-call(bf16[128,1024]{1,0:T(8,128)(2,1)} %tok_hbm.1, f32[8,128]{1,0:T(8,128)} %select_maximum_fusion.route_hbm, bf16[1,4096,1024]{2,1,0:T(8,128)(2,1)} %gate_hbm.1, bf16[1,4096,1024]{2,1,0:T(8,128)(2,1)} %up_hbm.1, bf16[1,2048,2048]{2,1,0:T(8,128)(2,1)} %down_hbm.1), custom_call_target="tpu_custom_call" | custom-call | tf_op jit(solution)/shard_map/pallas_call | solution.py:330
  86.2 1.9 %copy.8 = bf16[128,2048]{1,0:T(8,128)(2,1)} copy(bf16[128,2048]{1,0:T(8,128)(2,1)} %shard_map.64) | data formatting | bytes 1048576
where the time goes:
time: 88.3 us; the launch traced here: 88.1 us
  Pallas kernels  84.2 us (95%)
  other arithmetic  1.96 us (2%)
  local copies, waits for them, and re-layouts  1.88 us (2%)
    pallas_call x1, Pallas kernels, fused(): pl.pallas_call(functools.partial(kernel, S, E, top, cap), out_shape=jax.S...  84.2 us
    unnamed x1, local copies, waits for them, and re-layouts  1.88 us

commit v1 on v0

--- a/solution.py
+++ b/solution.py
@@ -58,9 +58,10 @@
 
 def kernel(
     S, E, top, cap,
-    tok_hbm, route_hbm, gate_hbm, up_hbm, down_hbm, out_ref,
-    T, R, WG, WU, WD, DISP, WR, X, G, U, HO, HX, PO, CS, CR, YS, YR, ZS, ZR, AG,
-    lsem, tsem, ssem, rsem, rrsem, hsem, csem, ysem, zsem, asem,
+    tok_hbm, ids_hbm, weights_hbm, gate_hbm, up_hbm, down_hbm, out_hbm,
+    T, IDS, RW, R, WG, WU, WD, DISP, WR, X, G, U, HO, HX, PO, CS, CR, ACC,
+    YS, YR, PF, ZS, ZR, ZX, ZO, OUT,
+    lsem, tsem, ssem, rsem, rrsem, hsem, csem, ysem, zsem, xsem, osem, dsem,
 ):
     s = lax.axis_index("section")
     e = lax.axis_index("expert")
@@ -79,8 +80,10 @@
 
     own = pltpu.make_async_copy(tok_hbm, T.at[s, pl.ds(pl.multiple_of(e * rows, rows), rows)], tsem.at[0])
     own.start()
-    route = pltpu.make_async_copy(route_hbm, R.at[e], tsem.at[1])
-    route.start()
+    ids = pltpu.make_async_copy(ids_hbm, IDS, tsem.at[1])
+    ids.start()
+    route_weights = pltpu.make_async_copy(weights_hbm, RW, tsem.at[2])
+    route_weights.start()
 
     barrier = pltpu.get_barrier_semaphore()
     partners = [{"section": lax.rem(s + j, S)} for j in range(1, S)]
@@ -100,17 +103,24 @@
     down_load = pltpu.make_async_copy(down_hbm.at[0], WD, lsem.at[2 * S])
 
     own.wait()
-    route.wait()
+    ids.wait()
+    route_weights.wait()
+    R[e] = jnp.zeros(R.shape[1:], jnp.float32)
+    R[e, 0:top, :] = IDS[...].astype(jnp.float32)
+    R[e, top : 2 * top, :] = RW[...]
     pl.semaphore_wait(barrier, len(partners))
 
-    def send(src, dst, recv, target):
+    def send(src, dst, recv, target, when=None):
         c = pltpu.make_async_remote_copy(
             src_ref=src, dst_ref=dst, send_sem=ssem.at[counter[0]], recv_sem=recv,
             device_id=target, device_id_type=MESH,
         )
         counter[0] += 1
-        pending.append(c)
-        c.start()
+        pending.append((when, c))
+        if when is None:
+            c.start()
+        else:
+            pl.when(when)(c.start)
 
     def arrived(ref, sem):
         pltpu.make_async_remote_copy(
@@ -234,7 +244,9 @@
     for j in others[:-1]:
         section_matmul(j, False)
     from_diag(others[-1])
-    groups = [oyc, oy, core, e]
+    near = e - lax.rem(e, 2)
+    far = lax.rem(near + 2, E)
+    groups = [far, far + 1, near, near + 1]
 
     def span(g):
         return pl.ds(pl.multiple_of(g * cap, cap), cap)
@@ -261,59 +273,146 @@
         cols = pl.ds(pl.multiple_of(n * otile, otile), otile)
         PO[:, cols] = jnp.dot(HO[...], WD[own_units, cols], preferred_element_type=jnp.float32)
 
-    quarter = rows // S
-
-    def lines(k):
-        return pl.ds(pl.multiple_of(k * quarter, quarter), quarter)
-
-    for i, g in enumerate(groups):
-        arrived(HX.at[span(g)], hsem.at[i])
-        if i == 1:
-            arrived(CR.at[0], csem.at[0])
-        if i == 3:
-            arrived(CR.at[1], csem.at[1])
-
-        @pl.loop(0, outs // otile)
+    side = lax.rem(e, 2)
+    part = outs // 2
+    chunks = YS.shape[1]
+    width = part // chunks
+    mine, theirs = side * part, (1 - side) * part
+    inner = (s == 1) | (s == 2)
+    outer = (s == 0) | (s == 3)
+    in_sec = jnp.where(s == 0, 1, 2)
+    cross = 3 - s
+    out_sec = jnp.where(s == 1, 0, 3)
+
+    def half(g, base, put):
+        @pl.loop(0, part // otile)
         def _(n):
-            cols = pl.ds(pl.multiple_of(n * otile, otile), otile)
+            cols = pl.ds(pl.multiple_of(base + n * otile, otile), otile)
             v = PO[span(g), cols] + jnp.dot(
                 HX[span(g), :], WD[other_units, cols], preferred_element_type=jnp.float32
             )
             v = (v * WR[g][:, 0:1]).astype(jnp.bfloat16)
             v = lax.dot_general(DISP[g], v, (((0,), (0,)), ((), ())), preferred_element_type=jnp.float32)
-            if i % 2 == 0:
-                CS[i // 2, :, cols] = v.astype(jnp.bfloat16)
-            elif i == 1:
-                YS[:, cols] = (v + CR[0, :, cols].astype(jnp.float32)).astype(jnp.bfloat16)
-            else:
-                G[0:rows, cols] = v + CR[1, :, cols].astype(jnp.float32)
-
-        if i % 2 == 0:
-            send(CS.at[i // 2], CR.at[i // 2], csem.at[i // 2], to_core)
-        elif i == 1:
-            for j in others + [0]:
-                send(YS.at[lines(sec[j])], YR.at[lines(sec[j])], ysem.at[j], to_y)
-
-    def joined(j):
-        arrived(YR.at[lines(sec[j])], ysem.at[j])
-        return G[lines(sec[j]), 0:outs] + YR[lines(sec[j]), :].astype(jnp.float32)
-
-    for j in others:
-        ZS[lines(sec[j]), :] = joined(j).astype(jnp.bfloat16)
-        send(ZS.at[lines(sec[j])], ZR.at[s], zsem.at[s], {"section": sec[j]})
-    total = joined(0)
-    for j in order[1:]:
-        arrived(ZR.at[sec[j]], zsem.at[sec[j]])
-    for j in order[1:]:
-        total = total + ZR[sec[j]].astype(jnp.float32)
-    AG[lines(s), :] = total.astype(jnp.bfloat16)
-    for j in order[1:]:
-        send(AG.at[lines(s)], AG.at[lines(s)], asem.at[s], {"section": sec[j]})
-    for j in order[1:]:
-        arrived(AG.at[lines(sec[j])], asem.at[sec[j]])
-    out_ref[...] = AG[...]
-    for c in pending:
-        c.wait_send()
+            put(pl.ds(pl.multiple_of(n * otile, otile), otile), v)
+
+    def to_partner(i):
+        def put(cols, v):
+            CS[i, :, cols] = v.astype(jnp.bfloat16)
+
+        half(groups[i], theirs, put)
+        send(CS.at[i], CR.at[i], csem.at[i], to_core)
+
+    def keep(i):
+        def put(cols, v):
+            ACC[i, :, cols] = v
+
+        half(groups[i], mine, put)
+        arrived(CR.at[i], csem.at[i])
+
+    def piece(i, n):
+        cols = slice(n * width, (n + 1) * width)
+        return ACC[i, :, cols] + CR[i, :, cols].astype(jnp.float32)
+
+    def to_neighbour(i):
+        for n in range(chunks):
+            YS[i, n] = piece(i, n).astype(jnp.bfloat16)
+            send(YS.at[i, n], YR.at[i, n], ysem.at[i, n], to_y)
+
+    def first(a, n):
+        arrived(YR.at[a, n], ysem.at[a, n])
+        total = piece(2 + a, n) + YR[a, n].astype(jnp.float32)
+
+        @pl.when(outer)
+        def _():
+            ZS[a, n] = total.astype(jnp.bfloat16)
+
+        @pl.when(inner)
+        def _():
+            PF[a, n] = total
+
+        send(ZS.at[a, n], ZR.at[a, n], zsem.at[a, n], {"section": in_sec}, outer)
+
+    def second(a, n):
+        @pl.when(inner)
+        def _():
+            arrived(ZR.at[a, n], zsem.at[a, n])
+            ZS[a, n] = (PF[a, n] + ZR[a, n].astype(jnp.float32)).astype(jnp.bfloat16)
+
+        send(ZS.at[a, n], ZX.at[a, n], xsem.at[a, n], {"section": cross}, inner)
+
+    drains = []
+
+    def drain(h, n, k):
+        cols = pl.ds(pl.multiple_of(h * part + n * width, width), width)
+        c = pltpu.make_async_copy(OUT.at[h, n], out_hbm.at[:, cols], dsem.at[k, n])
+        c.start()
+        drains.append(c)
+
+    def third(a, n):
+        @pl.when(inner)
+        def _():
+            arrived(ZX.at[a, n], xsem.at[a, n])
+            total = (ZS[a, n].astype(jnp.float32) + ZX[a, n].astype(jnp.float32)).astype(jnp.bfloat16)
+            ZO[a, n] = total
+
+            @pl.when(side == a)
+            def _():
+                OUT[side, n] = total
+
+        send(ZO.at[a, n], OUT.at[side, n], osem.at[side, n], {"section": out_sec, "expert": near + a}, inner)
+        send(ZO.at[a, n], OUT.at[side, n], osem.at[side, n], to_core, inner & (side != a))
+
+    def hidden_in(i):
+        arrived(HX.at[span(groups[i])], hsem.at[i])
+
+    for i in (0, 1):
+        hidden_in(i)
+        to_partner(i)
+        keep(i)
+        to_neighbour(i)
+    hidden_in(2)
+    to_partner(2)
+    keep(2)
+    steps = [functools.partial(second, 0, n) for n in range(chunks)]
+    for n in range(chunks):
+        first(0, n)
+    cut = chunks // 4
+    for f in steps[:cut]:
+        f()
+    hidden_in(3)
+    to_partner(3)
+    for f in steps[cut : 2 * cut]:
+        f()
+    keep(3)
+    for n in range(chunks):
+        first(1, n)
+    steps = steps[2 * cut :] + [functools.partial(third, 0, n) for n in range(chunks)]
+    lag = chunks // 2
+    for n in range(chunks + lag):
+        if n < chunks:
+            for f in steps[n * len(steps) // chunks : (n + 1) * len(steps) // chunks]:
+                f()
+            second(1, n)
+        if n >= lag:
+            third(1, n - lag)
+
+    for n in range(chunks):
+
+        @pl.when(outer)
+        def _():
+            arrived(OUT.at[side, n], osem.at[side, n])
+
+        drain(side, n, 0)
+    for n in range(chunks):
+        arrived(OUT.at[1 - side, n], osem.at[1 - side, n])
+        drain(1 - side, n, 1)
+    for c in drains:
+        c.wait()
+    for when, c in pending:
+        if when is None:
+            c.wait_send()
+        else:
+            pl.when(when)(c.wait_send)
 
 
 def fused(tokens, route_ids, route_weights, gate_weight, up_weight, down_weight):
@@ -322,58 +421,67 @@
     top = route_ids.shape[1]
     cap = 3 * rows * top // (2 * E)
     units, outs = gate_weight.shape[2], down_weight.shape[2]
-    table = jnp.concatenate([route_ids.T.astype(jnp.float32), route_weights.T], axis=0)
-    table = jnp.pad(table, ((0, -table.shape[0] % 8), (0, 0)))
+    table_rows = -(-2 * top // 8) * 8
     bf, f32 = jnp.bfloat16, jnp.float32
     dma = pltpu.SemaphoreType.DMA
-    sends = 128
+    sends = 256
+    part, chunks = outs // 2, outs // 256
+    grid = (2, chunks, rows, part // chunks)
     return pl.pallas_call(
         functools.partial(kernel, S, E, top, cap),
         out_shape=jax.ShapeDtypeStruct((rows, outs), bf),
-        in_specs=[pl.BlockSpec(memory_space=pl.ANY)] * 5,
-        out_specs=pl.BlockSpec(memory_space=pltpu.VMEM),
+        in_specs=[pl.BlockSpec(memory_space=pl.ANY)] * 6,
+        out_specs=pl.BlockSpec(memory_space=pl.ANY),
         scratch_shapes=[
             pltpu.VMEM((S, E * rows, feat), bf),
-            pltpu.VMEM((E,) + table.shape, f32),
+            pltpu.VMEM((top, rows), jnp.int32),
+            pltpu.VMEM((top, rows), f32),
+            pltpu.VMEM((E, table_rows, rows), f32),
             pltpu.VMEM((S * feat, units), bf),
             pltpu.VMEM((S * feat, units), bf),
             pltpu.VMEM(down_weight.shape[1:], bf),
             pltpu.VMEM((E, cap, rows), bf),
             pltpu.VMEM((E, cap, 128), f32),
             pltpu.VMEM((E * cap, feat), bf),
-            pltpu.VMEM((E * cap, max(units, outs)), f32),
+            pltpu.VMEM((E * cap, units), f32),
             pltpu.VMEM((E * cap, units), f32),
             pltpu.VMEM((E * cap, units), bf),
             pltpu.VMEM((E * cap, units), bf),
             pltpu.VMEM((E * cap, outs), f32),
-            pltpu.VMEM((2, rows, outs), bf),
-            pltpu.VMEM((2, rows, outs), bf),
-            pltpu.VMEM((rows, outs), bf),
-            pltpu.VMEM((rows, outs), bf),
-            pltpu.VMEM((rows, outs), bf),
-            pltpu.VMEM((S, rows // S, outs), bf),
-            pltpu.VMEM((rows, outs), bf),
+            pltpu.VMEM((4, rows, part), bf),
+            pltpu.VMEM((4, rows, part), bf),
+            pltpu.VMEM((4, rows, part), f32),
+            pltpu.VMEM(grid, bf),
+            pltpu.VMEM(grid, bf),
+            pltpu.VMEM(grid, f32),
+            pltpu.VMEM(grid, bf),
+            pltpu.VMEM(grid, bf),
+            pltpu.VMEM(grid, bf),
+            pltpu.VMEM(grid, bf),
+            pltpu.VMEM(grid, bf),
             dma((2 * S + 1,)),
-            dma((2,)),
+            dma((3,)),
             dma((sends,)),
             dma((2 * E * S,)),
             dma((E,)),
             dma((4,)),
-            dma((2,)),
-            dma((S,)),
-            dma((S,)),
-            dma((S,)),
+            dma((4,)),
+            dma((2, chunks)),
+            dma((2, chunks)),
+            dma((2, chunks)),
+            dma((2, chunks)),
+            dma((2, chunks)),
         ],
         compiler_params=pltpu.CompilerParams(
             collective_id=0, has_side_effects=True, vmem_limit_bytes=60 * 1024 * 1024
         ),
-    )(tokens, table, gate_weight, up_weight, down_weight)
+    )(tokens, route_ids.T, route_weights.T, gate_weight, up_weight, down_weight)
 
 
 def shards(tokens, route_ids, route_weights, gate_weight, up_weight, down_weight):
     args = (tokens, route_ids, route_weights, gate_weight, up_weight, down_weight)
     pairs = lax.axis_size("expert") == 2 * 2 and lax.axis_size("seq") == 2
-    if pairs and lax.axis_size("section") > 2:
+    if pairs and lax.axis_size("section") == 4:
         return fused(*args)
     return plain(*args)
 

time: 88.3 us -> 82.2 us (0.931)
  the two profiles are of different devices: /device:TPU:2 before, /device:TPU:1 now
where the time goes in v1:
time: 82.2 us; the launch traced here: 82 us
  Pallas kernels  80.1 us (97%)
  local copies, waits for them, and re-layouts  1.88 us (2%)
    pallas_call x1, Pallas kernels, fused(): pl.pallas_call(functools.partial(kernel, S, E, top, cap), out_shape=jax.S...  80.1 us
    unnamed x1, local copies, waits for them, and re-layouts  1.88 us

profile of v1, /device:TPU:1, one launch (start us, length us, event | category | flops | bytes accessed | tf_op | source)
XLA Modules:
  0.0 82.0 jit_solution(5735154024983976477)
XLA Ops:
  0.0 80.1 %shard_map.64 = bf16[128,2048]{1,0:T(8,128)(2,1)} custom-call(bf16[128,1024]{1,0:T(8,128)(2,1)} %tok_hbm.1, s32[2,128]{1,0:T(2,128)} %bitcast.2, f32[2,128]{1,0:T(2,128)} %bitcast.3, bf16[1,4096,1024]{2,1,0:T(8,128)(2,1)} %gate_hbm.1, bf16[1,4096,1024]{2,1,0:T(8,128)(2,1)} %up_hbm.1, bf16[1,2048,2048]{2,1,0:T(8,128)(2,1)} %down_hbm.1), custom_call_target="tpu_custom_call" | custom-call | tf_op jit(solution)/shard_map/pallas_call | solution.py:430
  80.1 1.9 %copy.8 = bf16[128,2048]{1,0:T(8,128)(2,1)} copy(bf16[128,2048]{1,0:T(8,128)(2,1)} %shard_map.64) | data formatting | bytes 1048576

commit v2 on v1

v2 whole, which is shorter than its diff:
```python
import functools

import jax
import jax.numpy as jnp
from jax import lax
from jax.experimental import pallas as pl
from jax.experimental.pallas import tpu as pltpu
from jax.sharding import PartitionSpec as P

MESH = pl.DeviceIdType.MESH


def plain(tokens, route_ids, route_weights, gate_weight, up_weight, down_weight):
    experts = lax.axis_size("expert")
    tok_rows, top_count = route_ids.shape
    capacity = 3 * tok_rows * top_count // (2 * experts)
    rows_total = experts * capacity
    flat_ids = route_ids.reshape(-1)
    onehot = (flat_ids[:, None] == jnp.arange(experts, dtype=jnp.int32)[None, :]).astype(jnp.int32)
    earlier = jnp.cumsum(onehot, axis=0) - onehot
    slot_index = jnp.sum(earlier * onehot, axis=1)
    destination = flat_ids * capacity + slot_index
    matches = (jnp.arange(rows_total, dtype=jnp.int32)[:, None] == destination[None, :]).astype(
        jnp.bfloat16
    )
    dispatch = jnp.sum(matches.reshape(rows_total, tok_rows, top_count), axis=2)
    outgoing = jnp.dot(dispatch, tokens, preferred_element_type=jnp.float32).astype(jnp.bfloat16)
    received = lax.all_to_all(
        outgoing.reshape(experts, capacity, tokens.shape[1]),
        "expert",
        split_axis=0,
        concat_axis=0,
        tiled=True,
    )
    received = received.reshape(rows_total, tokens.shape[1])
    piece = lax.all_gather(received, "section", axis=1, tiled=True)
    gate = jnp.dot(piece, gate_weight[0], preferred_element_type=jnp.float32)
    up = jnp.dot(piece, up_weight[0], preferred_element_type=jnp.float32)
    hidden = (jax.nn.silu(gate) * up).astype(jnp.bfloat16)
    partial_value = jnp.dot(
        lax.all_gather(hidden, "seq", axis=1, tiled=True),
        down_weight[0],
        preferred_element_type=jnp.float32,
    )
    summed = lax.psum_scatter(partial_value, "section", scatter_dimension=1, tiled=True)
    expert_out = summed.astype(jnp.bfloat16).reshape(experts, capacity, summed.shape[1])
    returned = lax.all_to_all(
        expert_out, "expert", split_axis=0, concat_axis=0, tiled=True
    ).reshape(rows_total, summed.shape[1])
    picked = (
        jnp.take(returned, destination, axis=0)
        .astype(jnp.float32)
        .reshape(tok_rows, top_count, summed.shape[1])
    )
    mixed = jnp.sum(picked * route_weights[:, :, None], axis=1).astype(jnp.bfloat16)
    return lax.all_gather(mixed, "section", axis=1, tiled=True)


def kernel(
    S, E, top, cap,
    tok_hbm, ids_hbm, weights_hbm, gate_hbm, up_hbm, down_hbm, out_hbm,
    T, IDS, RW, R, WG, WU, WD, DISP, WR, G, U, HO, HX, PO, CS, CR, ACC,
    YS, YR, PF, ZS, ZR, ZX, ZO, OUT,
    lsem, tsem, ssem, rsem, rrsem, hsem, csem, ysem, zsem, xsem, osem, dsem,
):
    s = lax.axis_index("section")
    e = lax.axis_index("expert")
    q = lax.axis_index("seq")
    side = lax.rem(e, 2)
    core = e + 1 - 2 * side
    near = e - side
    far = lax.rem(near + 2, E)
    oy = lax.rem(e + 2, E)
    oyc = lax.rem(core + 2, E)
    oq = 1 - q
    rows = tok_hbm.shape[0]
    block_rows = rows // 2
    feat = tok_hbm.shape[1]
    units = gate_hbm.shape[2]
    outs = down_hbm.shape[2]
    inner = (s == 1) | (s == 2)
    outer = (s == 0) | (s == 3)
    in_sec = jnp.where(s == 0, 1, 2)
    cross = 3 - s
    out_sec = jnp.where(s == 1, 0, 3)

    own = pltpu.make_async_copy(tok_hbm, T.at[s, pl.ds(pl.multiple_of(e * rows, rows), rows)], tsem.at[0])
    own.start()
    ids = pltpu.make_async_copy(ids_hbm, IDS, tsem.at[1])
    ids.start()
    route_weights = pltpu.make_async_copy(weights_hbm, RW, tsem.at[2])
    route_weights.start()

    to_x, to_y, to_core = {"seq": oq}, {"expert": oy}, {"expert": core}
    up, down, skip = ({"section": lax.rem(s + j, S)} for j in (1, S - 1, 2))
    barrier = pltpu.get_barrier_semaphore()
    for p, when in (
        (to_core, None), (to_x, None), (to_y, None), ({"expert": oyc}, None),
        (skip, None), (up, s != S - 1), (down, s != 0),
    ):
        def signal(p=p):
            pl.semaphore_signal(barrier, inc=1, device_id=p, device_id_type=MESH)

        if when is None:
            signal()
        else:
            pl.when(when)(signal)

    step = 1 + 2 * lax.rem(s, 2)
    sec = [s, lax.rem(s + 2, S), lax.rem(s + step, S), lax.rem(s + S - step, S)]
    bands = [pl.ds(pl.multiple_of(k * feat, feat), feat) for k in sec]
    loads = [
        (
            pltpu.make_async_copy(gate_hbm.at[0, band], WG.at[band], lsem.at[2 * i]),
            pltpu.make_async_copy(up_hbm.at[0, band], WU.at[band], lsem.at[2 * i + 1]),
        )
        for i, band in enumerate(bands)
    ]
    down_load = pltpu.make_async_copy(down_hbm.at[0], WD, lsem.at[2 * S])

    own.wait()
    for pair in loads:
        for c in pair:
            c.start()
    down_load.start()
    ids.wait()
    route_weights.wait()
    R[e] = jnp.zeros(R.shape[1:], jnp.float32)
    R[e, 0:top, :] = IDS[...].astype(jnp.float32)
    R[e, top : 2 * top, :] = RW[...]
    pl.semaphore_wait(barrier, 6 + inner.astype(jnp.int32))

    def send(kind, src, dst, recv, target, when=None):
        c = pltpu.make_async_remote_copy(
            src_ref=src, dst_ref=dst, send_sem=ssem.at[kind], recv_sem=recv,
            device_id=target, device_id_type=MESH,
        )
        if when is None:
            c.start()
        else:
            pl.when(when)(c.start)

    def arrived(ref, sem):
        pltpu.make_async_remote_copy(
            src_ref=ref, dst_ref=ref, send_sem=ssem.at[0], recv_sem=sem,
            device_id={"seq": oq}, device_id_type=MESH,
        ).wait_recv()

    def sent(kind, ref):
        pltpu.make_async_remote_copy(
            src_ref=ref, dst_ref=ref, send_sem=ssem.at[kind], recv_sem=ssem.at[kind],
            device_id={"seq": oq}, device_id_type=MESH,
        ).wait_send()

    def chunk(group, part, k):
        return T.at[k, pl.ds(pl.multiple_of(group * rows + part * block_rows, block_rows), block_rows)]

    def slot(group, part, k):
        return rsem.at[(group * 2 + part) * S + k]

    def push(kind, group, part, k, target, when=None):
        send(kind, chunk(group, part, k), chunk(group, part, k), slot(group, part, k), target, when)

    def take(group, part, k):
        arrived(chunk(group, part, k), slot(group, part, k))

    for target in (to_core, {"expert": oyc}, to_y):
        send(3, R.at[e], R.at[e], rrsem.at[e], target)
    push(0, e, 1 - side, s, to_core)
    push(0, e, side, s, to_core)

    def nearest(n):
        push(2, near + n, side, s, up, s != S - 1)
        push(2, near + n, side, s, down, s != 0)

    for n in (0, 1):

        @pl.when(side != n)
        def _():
            take(near + n, side, s)

        push(2, near + n, side, s, skip)
        if n == 0:
            nearest(n)
        push(1, near + n, side, s, to_y)

    me = e.astype(jnp.float32)
    before = (
        lax.broadcasted_iota(jnp.int32, (rows, rows), 0) < lax.broadcasted_iota(jnp.int32, (rows, rows), 1)
    ).astype(jnp.float32).astype(jnp.bfloat16)

    def dispatch(g):
        table = R[g]
        named = jnp.zeros((1, rows), jnp.float32)
        weight = jnp.zeros((1, rows), jnp.float32)
        for n in range(top):
            hit = (table[n : n + 1, :] == me).astype(jnp.float32)
            named = named + hit
            weight = weight + hit * table[top + n : top + n + 1, :]
        rank = jnp.dot(
            jnp.broadcast_to(named, (8, rows)).astype(jnp.bfloat16), before, preferred_element_type=jnp.float32
        )[0:1, :]
        place = lax.broadcasted_iota(jnp.int32, (cap, rows), 0).astype(jnp.float32)
        match = jnp.where(place == rank, 1.0, 0.0) * named
        DISP[g] = match.astype(jnp.bfloat16)
        WR[g] = jnp.broadcast_to(jnp.sum(match * weight, axis=1, keepdims=True), (cap, WR.shape[2]))

    def z_in(n, i, when=None):
        if when is not None:
            pl.when(when)(functools.partial(z_in, n, i))
            return
        take(near + n, side, sec[i])
        if i == 1:
            push(2, near + n, side, sec[i], {"section": out_sec}, inner)
        push(1, near + n, side, sec[i], to_y)
        push(0, near + n, side, sec[i], to_core)

    def y_in(n, i):
        take(far + n, side, sec[i])
        push(0, far + n, side, sec[i], to_core)

    groups = [near, far, near + 1, far + 1]
    loaded = set()

    def span(g):
        return pl.ds(pl.multiple_of(g * cap, cap), cap)

    def block(m, i):
        g, k = groups[m], sec[i]
        if m % 2 == 0 and i == 0:

            @pl.when(side != m // 2)
            def _():
                take(g, 1 - side, k)
        else:
            take(g, 1 - side, k)
        if i not in loaded:
            loaded.add(i)
            for c in loads[i]:
                c.wait()
        lines = pl.ds(pl.multiple_of(g * rows, rows), rows)
        for W, A in ((WG, G), (WU, U)):
            v = jnp.dot(T[k, lines, :], W[bands[i], :], preferred_element_type=jnp.float32)
            if i == 0:
                A[m] = v
            else:
                A[m] = A[m] + v

    def hidden_out(m):
        a = G[m]
        h = (a / (1.0 + jnp.exp(-a)) * U[m]).astype(jnp.bfloat16)
        HO[m] = jnp.dot(DISP[groups[m]], h, preferred_element_type=jnp.float32).astype(jnp.bfloat16)
        send(4, HO.at[m], HX.at[m], hsem.at[m], to_x)

    own_units = pl.ds(pl.multiple_of(q * units, units), units)
    other_units = pl.ds(pl.multiple_of(oq * units, units), units)
    part = outs // 2
    chunks = YS.shape[1]
    width = part // chunks
    mine, theirs = (pl.ds(pl.multiple_of(h * part, part), part) for h in (side, 1 - side))

    def ahead(m):
        if m == 1:
            down_load.wait()
        PO[m] = jnp.dot(HO[m], WD[own_units, :], preferred_element_type=jnp.float32)

    def half(m, cols):
        g = groups[m]
        v = PO[m, :, cols] + jnp.dot(HX[m], WD[other_units, cols], preferred_element_type=jnp.float32)
        v = (v * WR[g][:, 0:1]).astype(jnp.bfloat16)
        return lax.dot_general(DISP[g], v, (((0,), (0,)), ((), ())), preferred_element_type=jnp.float32)

    def to_partner(m):
        CS[m] = half(m, theirs).astype(jnp.bfloat16)
        send(5, CS.at[m], CR.at[m], csem.at[m], to_core)

    def keep(m):
        ACC[m] = half(m, mine)
        arrived(CR.at[m], csem.at[m])

    def piece(m, n):
        cols = slice(n * width, (n + 1) * width)
        return ACC[m, :, cols] + CR[m, :, cols].astype(jnp.float32)

    def to_neighbour(b):
        for n in range(chunks):
            YS[b, n] = piece(2 * b + 1, n).astype(jnp.bfloat16)
            send(6, YS.at[b, n], YR.at[b, n], ysem.at[b, n], to_y)

    def first(a, n):
        arrived(YR.at[a, n], ysem.at[a, n])
        total = piece(2 * a, n) + YR[a, n].astype(jnp.float32)

        @pl.when(outer)
        def _():
            ZS[a, n] = total.astype(jnp.bfloat16)

        @pl.when(inner)
        def _():
            PF[a, n] = total

        send(7, ZS.at[a, n], ZR.at[a, n], zsem.at[a, n], {"section": in_sec}, outer)

    def second(a, n):
        @pl.when(inner)
        def _():
            arrived(ZR.at[a, n], zsem.at[a, n])
            ZS[a, n] = (PF[a, n] + ZR[a, n].astype(jnp.float32)).astype(jnp.bfloat16)

        send(7, ZS.at[a, n], ZX.at[a, n], xsem.at[a, n], {"section": cross}, inner)

    def drain(h):
        for n in range(chunks):
            cols = pl.ds(pl.multiple_of(h * part + n * width, width), width)
            out_hbm[:, cols] = OUT[h, n]

    def third(a, n):
        @pl.when(inner)
        def _():
            arrived(ZX.at[a, n], xsem.at[a, n])
            total = (ZS[a, n].astype(jnp.float32) + ZX[a, n].astype(jnp.float32)).astype(jnp.bfloat16)
            ZO[a, n] = total

            @pl.when(side == a)
            def _():
                OUT[side, n] = total

        send(8, ZO.at[a, n], OUT.at[side, n], osem.at[side], {"section": out_sec, "expert": near + a}, inner)
        send(9, ZO.at[a, n], OUT.at[side, n], osem.at[side], to_core, inner & (side != a))

    def hidden_in(m):
        arrived(HX.at[m], hsem.at[m])

    block(0, 0)
    for g in (core, oy, oyc):
        arrived(R.at[g], rrsem.at[g])
    block(2, 0)
    dispatch(near)
    dispatch(far)
    dispatch(near + 1)
    dispatch(far + 1)
    y_in(0, 0)
    z_in(0, 1)
    nearest(1)
    z_in(0, 2)
    block(1, 0)
    y_in(1, 0)
    block(0, 1)
    block(0, 2)
    z_in(0, 3)
    z_in(1, 1, inner)
    block(3, 0)
    y_in(0, 1)
    block(0, 3)
    hidden_out(0)
    block(1, 1)
    z_in(1, 1, outer)
    z_in(1, 2)
    y_in(0, 2)
    block(2, 1)
    z_in(1, 3, inner)
    y_in(0, 3)
    z_in(1, 3, outer)
    block(1, 2)
    block(2, 2)
    block(1, 3)
    hidden_out(1)
    y_in(1, 1)
    block(2, 3)
    hidden_out(2)
    ahead(1)
    block(3, 1)
    ahead(0)
    y_in(1, 2)
    hidden_in(0)
    to_partner(0)
    block(3, 2)
    y_in(1, 3)
    keep(0)
    block(3, 3)
    hidden_out(3)
    hidden_in(1)
    to_partner(1)
    keep(1)
    to_neighbour(0)
    ahead(2)
    ahead(3)
    hidden_in(2)
    to_partner(2)
    keep(2)
    cut = chunks // 2
    for n in range(cut):
        first(0, n)
    hidden_in(3)
    to_partner(3)
    for n in range(cut, cut + 2):
        first(0, n)
    keep(3)
    to_neighbour(1)
    for n in range(cut + 2, chunks):
        first(0, n)
    for n in range(chunks):
        second(0, n)
    for n in range(chunks + 2 * cut):
        if n < chunks:
            third(0, n)
            first(1, n)
        if cut <= n < chunks + cut:
            second(1, n - cut)
        if n >= 2 * cut:
            third(1, n - 2 * cut)

    @pl.when(outer)
    def _():
        arrived(OUT.at[side], osem.at[side])

    drain(side)
    arrived(OUT.at[1 - side], osem.at[1 - side])
    drain(1 - side)
    sent(0, T.at[0:2])
    sent(1, T.at[0])
    sent(3, R.at[0:3])
    sent(4, HO)
    sent(5, CS)
    sent(6, YS)
    sent(7, ZS)

    @pl.when(outer)
    def _():
        sent(2, T.at[0, 0 : 2 * rows])

    @pl.when(inner)
    def _():
        sent(2, T.at[0])
        sent(8, ZO)
        sent(9, ZO.at[0])


def fused(tokens, route_ids, route_weights, gate_weight, up_weight, down_weight):
    S, E = lax.axis_size("section"), lax.axis_size("expert")
    rows, feat = tokens.shape
    top = route_ids.shape[1]
    cap = 3 * rows * top // (2 * E)
    units, outs = gate_weight.shape[2], down_weight.shape[2]
    table_rows = -(-2 * top // 8) * 8
    bf, f32 = jnp.bfloat16, jnp.float32
    dma = pltpu.SemaphoreType.DMA
    sends = 10
    part, chunks = outs // 2, outs // 256
    grid = (2, chunks, rows, part // chunks)
    return pl.pallas_call(
        functools.partial(kernel, S, E, top, cap),
        out_shape=pltpu.VMEM((rows, outs), bf),
        in_specs=[pl.BlockSpec(memory_space=pl.ANY)] * 6,
        out_specs=pl.BlockSpec(memory_space=pltpu.VMEM),
        scratch_shapes=[
            pltpu.VMEM((S, E * rows, feat), bf),
            pltpu.VMEM((top, rows), jnp.int32),
            pltpu.VMEM((top, rows), f32),
            pltpu.VMEM((E, table_rows, rows), f32),
            pltpu.VMEM((S * feat, units), bf),
            pltpu.VMEM((S * feat, units), bf),
            pltpu.VMEM(down_weight.shape[1:], bf),
            pltpu.VMEM((E, cap, rows), bf),
            pltpu.VMEM((E, cap, 128), f32),
            pltpu.VMEM((E, rows, units), f32),
            pltpu.VMEM((E, rows, units), f32),
            pltpu.VMEM((E, cap, units), bf),
            pltpu.VMEM((E, cap, units), bf),
            pltpu.VMEM((E, cap, outs), f32),
            pltpu.VMEM((4, rows, part), bf),
            pltpu.VMEM((4, rows, part), bf),
            pltpu.VMEM((4, rows, part), f32),
            pltpu.VMEM(grid, bf),
            pltpu.VMEM(grid, bf),
            pltpu.VMEM(grid, f32),
            pltpu.VMEM(grid, bf),
            pltpu.VMEM(grid, bf),
            pltpu.VMEM(grid, bf),
            pltpu.VMEM(grid, bf),
            pltpu.VMEM(grid, bf),
            dma((2 * S + 1,)),
            dma((3,)),
            dma((sends,)),
            dma((2 * E * S,)),
            dma((E,)),
            dma((4,)),
            dma((4,)),
            dma((2, chunks)),
            dma((2, chunks)),
            dma((2, chunks)),
            dma((2,)),
            dma((1,)),
        ],
        compiler_params=pltpu.CompilerParams(
            collective_id=0, has_side_effects=True, vmem_limit_bytes=60 * 1024 * 1024
        ),
    )(tokens, route_ids.T, route_weights.T, gate_weight, up_weight, down_weight)


def shards(tokens, route_ids, route_weights, gate_weight, up_weight, down_weight):
    args = (tokens, route_ids, route_weights, gate_weight, up_weight, down_weight)
    pairs = lax.axis_size("expert") == 2 * 2 and lax.axis_size("seq") == 2
    if pairs and lax.axis_size("section") == 4:
        return fused(*args)
    return plain(*args)


def solution(mesh):
    in_specs = (
        P("expert", "section"),
        P("expert", None),
        P("expert", None),
        P("expert", None, ("section", "seq")),
        P("expert", None, ("section", "seq")),
        P("expert", "section", "seq"),
    )
    out_specs = P("expert", "seq")
    return jax.shard_map(shards, mesh=mesh, in_specs=in_specs, out_specs=out_specs, check_vma=False)
```

time: 82.2 us -> 62.3 us (0.76)
  Pallas kernels: 80.1 us -> 61.3 us
  local copies, waits for them, and re-layouts: 1.88 us -> 0.8 us
    pallas_call x1, Pallas kernels: 80.1 us -> 61.3 us  [fused(): pl.pallas_call(functools.partial(kernel, S, E, top, cap), out_shape=pltpu...]
    unnamed x1, local copies, waits for them, and re-layouts: 1.88 us -> 0.8 us
where the time goes in v2:
time: 62.3 us; the launch traced here: 62.1 us
  Pallas kernels  61.3 us (98%)
  local copies, waits for them, and re-layouts  0.8 us (1%)
    pallas_call x1, Pallas kernels, fused(): pl.pallas_call(functools.partial(kernel, S, E, top, cap), out_shape=pltpu...  61.3 us

profile of v2, /device:TPU:1, one launch (start us, length us, event | category | flops | bytes accessed | tf_op | source)
XLA Modules:
  0.0 62.1 jit_solution(7005544370623637573)
XLA Ops:
  0.0 61.3 %shard_map.64 = bf16[128,2048]{1,0:T(8,128)(2,1)S(1)} custom-call(bf16[128,1024]{1,0:T(8,128)(2,1)} %tok_hbm.1, s32[2,128]{1,0:T(2,128)} %bitcast.2, f32[2,128]{1,0:T(2,128)} %bitcast.3, bf16[1,4096,1024]{2,1,0:T(8,128)(2,1)} %gate_hbm.1, bf16[1,4096,1024]{2,1,0:T(8,128)(2,1)} %up_hbm.1, bf16[1,2048,2048]{2,1,0:T(8,128)(2,1)} %down_hbm.1), custom_call_target="tpu_custom_call" | custom-call | tf_op jit(solution)/shard_map/pallas_call | solution.py:451
  61.3 0.8 %copy.8 = bf16[128,2048]{1,0:T(8,128)(2,1)} copy(bf16[128,2048]{1,0:T(8,128)(2,1)S(1)} %shard_map.64) | data formatting | bytes 1048576

commit v3 on v2

--- a/solution.py
+++ b/solution.py
@@ -152,26 +152,31 @@
             device_id={"seq": oq}, device_id_type=MESH,
         ).wait_send()
 
-    def chunk(group, part, k):
-        return T.at[k, pl.ds(pl.multiple_of(group * rows + part * block_rows, block_rows), block_rows)]
-
-    def slot(group, part, k):
-        return rsem.at[(group * 2 + part) * S + k]
-
-    def push(kind, group, part, k, target, when=None):
-        send(kind, chunk(group, part, k), chunk(group, part, k), slot(group, part, k), target, when)
-
-    def take(group, part, k):
-        arrived(chunk(group, part, k), slot(group, part, k))
+    lot = block_rows // 2
+
+    def chunk(group, part, k, h):
+        return T.at[k, pl.ds(pl.multiple_of(group * rows + part * block_rows + h * lot, lot), lot)]
+
+    def slot(group, part, k, h):
+        return rsem.at[((group * 2 + part) * S + k) * 2 + h]
+
+    def push(kind, group, part, k, target, when=None, lots=(0, 1)):
+        for h in lots:
+            c = chunk(group, part, k, h)
+            send(kind, c, c, slot(group, part, k, h), target, when)
+
+    def take(group, part, k, lots=(0, 1)):
+        for h in lots:
+            arrived(chunk(group, part, k, h), slot(group, part, k, h))
 
     for target in (to_core, {"expert": oyc}, to_y):
         send(3, R.at[e], R.at[e], rrsem.at[e], target)
     push(0, e, 1 - side, s, to_core)
     push(0, e, side, s, to_core)
 
-    def nearest(n):
-        push(2, near + n, side, s, up, s != S - 1)
-        push(2, near + n, side, s, down, s != 0)
+    def nearest(n, lots=(0, 1)):
+        push(2, near + n, side, s, up, s != S - 1, lots)
+        push(2, near + n, side, s, down, s != 0, lots)
 
     for n in (0, 1):
 
@@ -205,19 +210,21 @@
         DISP[g] = match.astype(jnp.bfloat16)
         WR[g] = jnp.broadcast_to(jnp.sum(match * weight, axis=1, keepdims=True), (cap, WR.shape[2]))
 
-    def z_in(n, i, when=None):
+    def z_in(n, i, when=None, lots=(0, 1)):
         if when is not None:
-            pl.when(when)(functools.partial(z_in, n, i))
+            pl.when(when)(functools.partial(z_in, n, i, None, lots))
             return
-        take(near + n, side, sec[i])
-        if i == 1:
-            push(2, near + n, side, sec[i], {"section": out_sec}, inner)
-        push(1, near + n, side, sec[i], to_y)
-        push(0, near + n, side, sec[i], to_core)
-
-    def y_in(n, i):
-        take(far + n, side, sec[i])
-        push(0, far + n, side, sec[i], to_core)
+        for h in lots:
+            take(near + n, side, sec[i], (h,))
+            if i == 1:
+                push(2, near + n, side, sec[i], {"section": out_sec}, inner, (h,))
+            push(1, near + n, side, sec[i], to_y, None, (h,))
+            push(0, near + n, side, sec[i], to_core, None, (h,))
+
+    def y_in(n, i, lots=(0, 1)):
+        for h in lots:
+            take(far + n, side, sec[i], (h,))
+            push(0, far + n, side, sec[i], to_core, None, (h,))
 
     groups = [near, far, near + 1, far + 1]
     loaded = set()
@@ -340,49 +347,55 @@
     dispatch(near + 1)
     dispatch(far + 1)
     y_in(0, 0)
-    z_in(0, 1)
+    z_in(0, 1, None, (0,))
+    z_in(0, 2, None, (0,))
+    z_in(0, 1, None, (1,))
     nearest(1)
-    z_in(0, 2)
+    z_in(0, 2, None, (1,))
     block(1, 0)
     y_in(1, 0)
     block(0, 1)
+    z_in(0, 3, None, (0,))
     block(0, 2)
-    z_in(0, 3)
+    z_in(0, 3, None, (1,))
     z_in(1, 1, inner)
+    y_in(0, 1)
     block(3, 0)
-    y_in(0, 1)
     block(0, 3)
     hidden_out(0)
+    y_in(0, 2)
     block(1, 1)
-    z_in(1, 1, outer)
-    z_in(1, 2)
-    y_in(0, 2)
+    z_in(1, 1, outer, (0,))
+    z_in(1, 2, None, (0,))
+    y_in(0, 3, (0,))
+    block(1, 2)
+    z_in(1, 1, outer, (1,))
+    z_in(1, 2, None, (1,))
+    y_in(0, 3, (1,))
     block(2, 1)
-    z_in(1, 3, inner)
-    y_in(0, 3)
-    z_in(1, 3, outer)
-    block(1, 2)
-    block(2, 2)
     block(1, 3)
     hidden_out(1)
-    y_in(1, 1)
+    z_in(1, 3, None, (0,))
+    block(2, 2)
+    z_in(1, 3, None, (1,))
+    ahead(1)
     block(2, 3)
     hidden_out(2)
-    ahead(1)
+    y_in(1, 1)
+    ahead(0)
     block(3, 1)
-    ahead(0)
     y_in(1, 2)
     hidden_in(0)
     to_partner(0)
     block(3, 2)
     y_in(1, 3)
-    keep(0)
+    hidden_in(1)
+    to_partner(1)
     block(3, 3)
     hidden_out(3)
-    hidden_in(1)
-    to_partner(1)
     keep(1)
     to_neighbour(0)
+    keep(0)
     ahead(2)
     ahead(3)
     hidden_in(2)
@@ -482,7 +495,7 @@
             dma((2 * S + 1,)),
             dma((3,)),
             dma((sends,)),
-            dma((2 * E * S,)),
+            dma((4 * E * S,)),
             dma((E,)),
             dma((4,)),
             dma((4,)),

time: 62.3 us -> 60.8 us (0.976)
  Pallas kernels: 61.3 us -> 59.9 us
    pallas_call x1, Pallas kernels: 61.3 us -> 59.9 us  [fused(): pl.pallas_call(functools.partial(kernel, S, E, top, cap), out_shape=pltpu...]
where the time goes in v3:
time: 60.8 us; the launch traced here: 60.7 us
  Pallas kernels  59.9 us (99%)
  local copies, waits for them, and re-layouts  0.8 us (1%)
    pallas_call x1, Pallas kernels, fused(): pl.pallas_call(functools.partial(kernel, S, E, top, cap), out_shape=pltpu...  59.9 us

profile of v3, /device:TPU:1, one launch (start us, length us, event | category | flops | bytes accessed | tf_op | source)
XLA Modules:
  0.0 60.7 jit_solution(14346008331833742623)
XLA Ops:
  0.0 59.9 %shard_map.64 = bf16[128,2048]{1,0:T(8,128)(2,1)S(1)} custom-call(bf16[128,1024]{1,0:T(8,128)(2,1)} %tok_hbm.1, s32[2,128]{1,0:T(2,128)} %bitcast.2, f32[2,128]{1,0:T(2,128)} %bitcast.3, bf16[1,4096,1024]{2,1,0:T(8,128)(2,1)} %gate_hbm.1, bf16[1,4096,1024]{2,1,0:T(8,128)(2,1)} %up_hbm.1, bf16[1,2048,2048]{2,1,0:T(8,128)(2,1)} %down_hbm.1), custom_call_target="tpu_custom_call" | custom-call | tf_op jit(solution)/shard_map/pallas_call | solution.py:464
  59.9 0.8 %copy.8 = bf16[128,2048]{1,0:T(8,128)(2,1)} copy(bf16[128,2048]{1,0:T(8,128)(2,1)S(1)} %shard_map.64) | data formatting | bytes 1048576
